TPU v7x, 16 devices: a whole 2x2x2 slice. The times are simulated.
16 devices in a mesh: rep: 1, r: 2 (over z), s: 8 (over x, y, core).
Axes of the slice: x: 2, y: 2, z: 2, core: 2. Of those that a mesh axis runs over, the one named last changes fastest.
Arguments:
- x: bfloat16 [16, 4096, 1024], P(('rep', 'r', 's'))
- dy: bfloat16 [16, 4096, 1024], P(('rep', 'r', 's'))
- w_gate: bfloat16 [2, 1024, 2560], P(None, 's')
- w_up: bfloat16 [2, 1024, 2560], P(None, 's')
- w_down: bfloat16 [2, 2560, 1024], P(None, 's')
- m_w_gate: float32 [2, 1024, 2560], P(None, 's')
- m_w_up: float32 [2, 1024, 2560], P(None, 's')
- m_w_down: float32 [2, 2560, 1024], P(None, 's')
- v_w_gate: float32 [2, 1024, 2560], P(None, 's')
- v_w_up: float32 [2, 1024, 2560], P(None, 's')
- v_w_down: float32 [2, 2560, 1024], P(None, 's')
Outputs:
- output 1: bfloat16 [2, 1024, 2560], P('rep', 's')
- output 2: bfloat16 [2, 1024, 2560], P('rep', 's')
- output 3: bfloat16 [2, 2560, 1024], P('rep', 's')
- output 4: float32 [2, 1024, 2560], P('rep', 's')
- output 5: float32 [2, 1024, 2560], P('rep', 's')
- output 6: float32 [2, 2560, 1024], P('rep', 's')
- output 7: float32 [2, 1024, 2560], P('rep', 's')
- output 8: float32 [2, 1024, 2560], P('rep', 's')
- output 9: float32 [2, 2560, 1024], P('rep', 's')
All inputs are finite; a program needn't handle non-finite values.
Results may differ from a plain program's by a relative error of at most 0.022.
Values are sent between devices in bfloat16 or wider.
A program may use at most 2 GiB of HBM per device.

v0:
```python
import jax
import jax.numpy as jnp
from jax import lax
from jax.sharding import PartitionSpec as P

NAMES = ("w_gate", "w_up", "w_down")


def matmul(a, w):
    return jnp.dot(a, w, preferred_element_type=jnp.float32).astype(jnp.bfloat16)


def normed(h):
    wide = h.astype(jnp.float32)
    scale = lax.rsqrt(jnp.mean(wide**2, -1, keepdims=True) + 1e-6)
    return (wide * scale).astype(jnp.bfloat16)


def layer(h, w):
    a = normed(h)
    gate = jnp.dot(a, w["w_gate"], preferred_element_type=jnp.float32)
    up = jnp.dot(a, w["w_up"], preferred_element_type=jnp.float32)
    return h + matmul((jax.nn.silu(gate) * up).astype(jnp.bfloat16), w["w_down"])


def adamw(w, m, v, g):
    m = 0.9 * m + 0.1 * g
    v = 0.95 * v + 0.05 * g * g
    step = m * lax.rsqrt(v + 1e-8) + 0.1 * w
    return (w - 0.02 * step).astype(jnp.bfloat16), m, v


def clipped(gradients, sum_of_squares, count):
    factor = jnp.minimum(1.0, 0.5 * lax.rsqrt(sum_of_squares / count + 1e-30))
    return [g * factor for g in gradients]


def solution(mesh):
    def fetched(weights, number):
        return {name: lax.all_gather(w[number], "s", axis=0, tiled=True) for name, w in zip(NAMES, weights, strict=True)}

    def summed(term):
        return lax.psum(lax.psum_scatter(term, "s", scatter_dimension=0, tiled=True), "r")

    def step(x, dy, *arrays):
        weights, m, v = (arrays[i : i + 3] for i in (0, 3, 6))
        layers = weights[0].shape[0]
        h, kept = x[0], []
        for number in range(layers):
            kept.append(h)
            h = layer(h, fetched(weights, number))
        by_h, mine = dy[0], [None] * layers
        for number in reversed(range(layers)):
            _, back = jax.vjp(lambda w, h: layer(h, w), fetched(weights, number), kept[number])
            by_w, by_h = back(by_h)
            mine[number] = [summed(by_w[name]) for name in NAMES]
        gradients = [jnp.stack([mine[number][i] for number in range(layers)]).astype(jnp.float32) for i in range(3)]
        squares = lax.psum(sum(jnp.sum(g * g) for g in gradients), "s")
        gradients = clipped(gradients, squares, lax.psum(1, "s") * sum(g.size for g in gradients))
        new = [adamw(w.astype(jnp.float32), m, v, g) for w, m, v, g in zip(weights, m, v, gradients, strict=True)]
        return tuple(one[which] for which in range(3) for one in new)

    states, cut = P(("rep", "r", "s"), None, None), P(None, "s", None)
    return jax.shard_map(
        step,
        mesh=mesh,
        in_specs=(states, states) + (cut,) * 9,
        out_specs=(P("rep", "s", None),) * 9,
        check_vma=False,
    )
```

profile of v0, /device:TPU:0, one launch (start us, length us, event | category | flops | bytes accessed | tf_op | source)
XLA Modules:
  0.0 878.7 jit_solution(11221837161887884912)
XLA Ops:
  16.5 11.5 %copy.20 = bf16[1,4096,1024]{1,2,0:T(8,128)(2,1)} copy(bf16[1,4096,1024]{2,1,0:T(8,128)(2,1)} %param.11) | data formatting | bytes 16777216 | tf_op args[0]
  28.0 5.1 fusion.15
  33.1 11.5 %copy.21 = bf16[1,4096,1024]{1,2,0:T(8,128)(2,1)} copy(bf16[1,4096,1024]{2,1,0:T(8,128)(2,1)} %param.12) | data formatting | bytes 16777216 | tf_op args[1]
  44.5 5.7 all-gather.13.cloned.1.call-done
  50.2 29.7 %fusion.44 = f32[4096,2560]{1,0:T(8,128)} fusion(bf16[1,4096,1024]{1,2,0:T(8,128)(2,1)} %copy.20, f32[4096]{0:T(1024)S(1)} %add_rsqrt_fusion, bf16[1,1024,2560]{2,1,0:T(8,128)(2,1)} %all-gather.13.cloned.1.call-done), kind=kOutput, calls=%fused_computation.54 | convolution fusion | flops 21487419392 | bytes 55590912 | tf_op jit(solution)/shard_map/dot_general | solution.py:21
  79.9 9.7 %all-gather.15.cloned.1.call-done = bf16[1,1024,2560]{2,1,0:T(8,128)(2,1)} async-done(((bf16[1,128,2560]{2,1,0:T(8,128)(2,1)}), bf16[1,1024,2560]{2,1,0:T(8,128)(2,1)}) %all-gather.15.cloned.1.call-update) | async-done | bytes 5242896 | tf_op jit(solution)/shard_map/all_gather | solution.py:40
  89.6 50.3 %multiply_convert_fusion.1 = (bf16[4096,2560]{1,0:T(8,128)(2,1)}, f32[4096,2560]{1,0:T(8,128)}) fusion(f32[4096,2560]{1,0:T(8,128)} %fusion.44, bf16[1,1024,2560]{2,1,0:T(8,128)(2,1)} %all-gather.15.cloned.1.call-done, bf16[1,4096,1024]{1,2,0:T(8,128)(2,1)} %copy.20, f32[4096]{0:T(1024)S(1)} %add_rsqrt_fusion), kind=kOutput, calls=%fused_computation.17 | convolution fusion | flops 21550333952 | bytes 118505472 | tf_op jit(solution)/shard_map/dot_general | solution.py:22
  139.9 29.7 %fusion.19 = (f32[4096]{0:T(1024)S(1)}, bf16[4096,1024]{0,1:T(8,128)(2,1)}) fusion(bf16[4096,2560]{1,0:T(8,128)(2,1)} %get-tuple-element.30, bf16[1,2560,1024]{2,1,0:T(8,128)(2,1)} %all-gather.17.cloned.1.call-done, bf16[1,4096,1024]{1,2,0:T(8,128)(2,1)} %copy.20), kind=kOutput, calls=%fused_computation.37 | convolution fusion | flops 21495803904 | bytes 43008000 | tf_op jit(solution)/shard_map/dot_general | solution.py:10
  170.3 29.1 %convolution_convert_fusion.1 = bf16[4096,2560]{1,0:T(8,128)(2,1)} fusion(bf16[1,4096,1024]{2,1,0:T(8,128)(2,1)} %param.12, bf16[1,2560,1024]{2,1,0:T(8,128)(2,1)} %all-gather.21.cloned.1.call-done), kind=kOutput, calls=%fused_computation.27 | convolution fusion | flops 21485322240 | bytes 34603008 | tf_op jit(solution)/shard_map/transpose(jvp())/dot_general | solution.py:10
  199.5 8.1 all-gather.23.cloned.1.call-done
  207.5 29.7 %fusion.36 = f32[4096,2560]{1,0:T(8,128)} fusion(bf16[4096,1024]{0,1:T(8,128)(2,1)} %get-tuple-element.33, f32[4096]{0:T(1024)S(1)} %fusion.77, bf16[1,1024,2560]{2,1,0:T(8,128)(2,1)} %all-gather.23.cloned.1.call-done), kind=kOutput, calls=%fused_computation.51 | convolution fusion | flops 21487419392 | bytes 55590912 | tf_op jit(solution)/shard_map/jvp()/dot_general | solution.py:22
  237.2 9.6 %all-gather.19.cloned.1.call-done = bf16[1,1024,2560]{2,1,0:T(8,128)(2,1)} async-done(((bf16[1,128,2560]{2,1,0:T(8,128)(2,1)}), bf16[1,1024,2560]{2,1,0:T(8,128)(2,1)}) %all-gather.19.cloned.1.call-update) | async-done | bytes 5242896 | tf_op jit(solution)/shard_map/all_gather | solution.py:40
  246.8 58.5 %fusion.2 = (bf16[4096,2560]{1,0:T(8,128)(2,1)}, f32[4096,2560]{1,0:T(8,128)}) fusion(f32[4096,2560]{1,0:T(8,128)} %fusion.36, bf16[4096,2560]{1,0:T(8,128)(2,1)} %convolution_convert_fusion.1, bf16[1,1024,2560]{2,1,0:T(8,128)(2,1)} %all-gather.19.cloned.1.call-done, bf16[4096,1024]{0,1:T(8,128)(2,1)} %get-tuple-element.33, f32[4096]{0:T(1024)S(1)} %fusion.77), kind=kOutput, calls=%fused_computation.8 | convolution fusion | flops 21613248512 | bytes 139476992 | tf_op jit(solution)/shard_map/jvp()/dot_general | solution.py:21
  305.4 26.3 %fusion.49 = bf16[4096,1024]{0,1:T(8,128)(2,1)} fusion(bf16[4096,2560]{1,0:T(8,128)(2,1)} %get-tuple-element.34, bf16[1,1024,2560]{2,1,0:T(8,128)(2,1)S(1)} %copy-done.18), kind=kOutput, calls=%fused_computation.58 | convolution fusion | flops 21474836480 | bytes 34603008 | tf_op jit(solution)/shard_map/transpose(jvp())/dot_general | solution.py:21
  331.6 38.8 %fusion.21 = (f32[4096]{0:T(1024)S(1)}, bf16[4096,1024]{0,1:T(8,128)(2,1)}) fusion(bf16[4096,1024]{0,1:T(8,128)(2,1)} %get-tuple-element.33, bf16[4096,1024]{0,1:T(8,128)(2,1)} %fusion.49, bf16[1,1024,2560]{2,1,0:T(8,128)(2,1)} %all-gather.23.cloned.1.call-done, bf16[4096,2560]{1,0:T(8,128)(2,1)} %convolution_convert_fusion.1, ...), kind=kOutput, calls=%fused_computation.39 | convolution fusion | flops 21562912768 | bytes 93339648 | tf_op jit(solution)/shard_map/transpose(jvp())/dot_general | solution.py:22
  370.5 10.9 %fusion.22 = bf16[4096,1024]{0,1:T(8,128)(2,1)S(1)} fusion(bf16[4096,1024]{0,1:T(8,128)(2,1)} %get-tuple-element.33, bf16[4096,1024]{0,1:T(8,128)(2,1)} %get-tuple-element.37, bf16[1,4096,1024]{1,2,0:T(8,128)(2,1)} %copy.21, f32[4096]{0:T(1024)S(1)} %multiply_multiply_fusion.3, f32[4096]{0:T(1024)S(1)} %fusion.77), kind=kLoop, calls=%fused_computation.40 | loop fusion | flops 29360128 | bytes 33587200 | tf_op jit(solution)/shard_map/transpose(jvp())/add_any | solution.py:14
  381.5 3.2 copy-done
  384.7 26.5 %convolution_convert_fusion.2 = bf16[2560,1024]{1,0:T(8,128)(2,1)} fusion(bf16[4096,2560]{1,0:T(8,128)(2,1)} %get-tuple-element.30, bf16[4096,1024]{0,1:T(8,128)(2,1)S(1)} %fusion.22), kind=kOutput, calls=%fused_computation.49 | convolution fusion | flops 21477457920 | bytes 34603008 | tf_op jit(solution)/shard_map/transpose(jvp())/dot_general | solution.py:10
  411.3 36.3 %fusion.29 = bf16[2560,1024]{1,0:T(8,128)(2,1)} fusion(bf16[1,4096,1024]{2,1,0:T(8,128)(2,1)} %param.12, f32[4096,2560]{1,0:T(8,128)} %fusion.36, f32[4096,2560]{1,0:T(8,128)} %get-tuple-element.35), kind=kOutput, calls=%fused_computation.46 | convolution fusion | flops 21540372480 | bytes 97517568 | tf_op jit(solution)/shard_map/transpose(jvp())/dot_general | solution.py:10
  447.7 28.2 %convolution_convert_fusion = bf16[4096,2560]{1,0:T(8,128)(2,1)} fusion(bf16[4096,1024]{0,1:T(8,128)(2,1)} %copy-done, bf16[1,2560,1024]{2,1,0:T(8,128)(2,1)} %all-gather.17.cloned.1.call-done), kind=kOutput, calls=%fused_computation.26 | convolution fusion | flops 21485322240 | bytes 34603008 | tf_op jit(solution)/shard_map/transpose(jvp())/dot_general | solution.py:10
  475.9 37.1 %fusion.33 = bf16[1024,2560]{1,0:T(8,128)(2,1)} fusion(bf16[4096,2560]{1,0:T(8,128)(2,1)} %convolution_convert_fusion, f32[4096,2560]{1,0:T(8,128)} %fusion.44, bf16[1,4096,1024]{1,2,0:T(8,128)(2,1)} %copy.20, f32[4096]{0:T(1024)S(1)} %copy-done.17), kind=kOutput, calls=%fused_computation.48 | convolution fusion | flops 21552955392 | bytes 76562432 | tf_op jit(solution)/shard_map/transpose(jvp())/dot_general | solution.py:22
  513.1 37.5 %fusion.32 = bf16[1024,2560]{1,0:T(8,128)(2,1)} fusion(bf16[4096,2560]{1,0:T(8,128)(2,1)} %convolution_convert_fusion.1, bf16[4096,1024]{0,1:T(8,128)(2,1)} %get-tuple-element.33, f32[4096]{0:T(1024)S(1)} %copy-done.13, f32[4096,2560]{1,0:T(8,128)} %get-tuple-element.35), kind=kOutput, calls=%fused_computation.47 | convolution fusion | flops 21552955392 | bytes 76562432 | tf_op jit(solution)/shard_map/transpose(jvp())/dot_general | solution.py:22
  550.7 44.8 %fusion.26 = bf16[1024,2560]{1,0:T(8,128)(2,1)} fusion(f32[4096,2560]{1,0:T(8,128)} %fusion.44, f32[4096,2560]{1,0:T(8,128)} %get-tuple-element.31, bf16[4096,2560]{1,0:T(8,128)(2,1)} %convolution_convert_fusion, bf16[1,4096,1024]{1,2,0:T(8,128)(2,1)} %copy.20, f32[4096]{0:T(1024)S(1)} %copy-done.17), kind=kOutput, calls=%fused_computation.45 | convolution fusion | flops 21605384192 | bytes 118505472 | tf_op jit(solution)/shard_map/transpose(jvp())/dot_general | solution.py:21
  595.5 28.5 %convolution_convert_fusion.3 = bf16[1024,2560]{1,0:T(8,128)(2,1)} fusion(bf16[4096,2560]{1,0:T(8,128)(2,1)} %get-tuple-element.34, bf16[4096,1024]{0,1:T(8,128)(2,1)} %get-tuple-element.33, f32[4096]{0:T(1024)S(1)} %copy-done.13), kind=kOutput, calls=%fused_computation.50 | convolution fusion | flops 21487419392 | bytes 34619392 | tf_op jit(solution)/shard_map/transpose(jvp())/dot_general | solution.py:21
  624.2 52.5 %reduce-scatter.7.cloned.1.call-done = bf16[128,2560]{1,0:T(8,128)(2,1)} async-done(((bf16[1024,2560]{1,0:T(8,128)(2,1)}), bf16[128,2560]{1,0:T(8,128)(2,1)}) %reduce-scatter.7.cloned.1.call-update) | async-done | bytes 655376 | tf_op jit(solution)/shard_map/reduce_scatter | solution.py:43
  676.7 53.6 %reduce-scatter.9.cloned.1.call-done = bf16[128,2560]{1,0:T(8,128)(2,1)} async-done(((bf16[1024,2560]{1,0:T(8,128)(2,1)}), bf16[128,2560]{1,0:T(8,128)(2,1)}) %reduce-scatter.9.cloned.1.call-update) | async-done | bytes 655376 | tf_op jit(solution)/shard_map/reduce_scatter | solution.py:43
  730.3 101.7 %all-reduce.3.cloned.1.call-done = (bf16[1,128,2560]{2,1,0:T(8,128)(2,1)}, bf16[1,128,2560]{2,1,0:T(8,128)(2,1)}, bf16[1,128,2560]{2,1,0:T(8,128)(2,1)}, bf16[1,...) async-done(((bf16[1,128,2560]{2,1,0:T(8,128)(2,1)}, bf16[1,128,2560]{2,1,0:T(8,128)(2,1)}, bf16[1,128,2560]{2,1,0:T(8,128)(2,1)}, ...) | async-done | bytes 3932176 | tf_op jit(solution)/shard_map/psum | solution.py:43
  832.0 2.6 fusion.67
  834.6 2.7 fusion.66
  841.8 13.8 %psum.55 = f32[]{:T(128)} all-reduce(f32[]{:T(128)S(6)} %add.111), channel_id=1, replica_groups=mesh['rep'=1,'r'=2,'s'=8] {'s'}, use_global_device_ids=true, to_apply=%region_18.19 | all-reduce | flops 1 | bytes 8 | tf_op jit(solution)/shard_map/psum | solution.py:58
  856.4 6.1 fusion.73
  865.5 6.2 fusion.64
  (76 shorter events, 15.8 us)
Async XLA Ops:
  7.2 43.0 %all-gather.13.cloned.1.call-start = ((), (), s32[]{:S(2)}) async-start(), calls=%async_computation.12 | async-start | bytes 5898240 | tf_op jit(solution)/shard_map/all_gather | solution.py:40
  9.7 79.9 %all-gather.15.cloned.1.call-start = ((), (), s32[]{:S(2)}) async-start(), calls=%async_computation.13 | async-start | bytes 5898240 | tf_op jit(solution)/shard_map/all_gather | solution.py:40
  12.2 127.8 %all-gather.17.cloned.1.call-start = ((), (), s32[]{:S(2)}) async-start(), calls=%async_computation.14 | async-start | bytes 5898240 | tf_op jit(solution)/shard_map/all_gather | solution.py:40
  14.7 155.7 %all-gather.21.cloned.1.call-start = ((), (), s32[]{:S(2)}) async-start(), calls=%async_computation.16 | async-start | bytes 5898240 | tf_op jit(solution)/shard_map/all_gather | solution.py:40
  15.3 192.3 %all-gather.23.cloned.1.call-start = ((), (), s32[]{:S(2)}) async-start(), calls=%async_computation.17 | async-start | bytes 5898240 | tf_op jit(solution)/shard_map/all_gather | solution.py:40
  15.8 231.0 %all-gather.19.cloned.1.call-start = ((), (), s32[]{:S(2)}) async-start(), calls=%async_computation.15 | async-start | bytes 5898240 | tf_op jit(solution)/shard_map/all_gather | solution.py:40
  16.4 607.7 %reduce-scatter.15.cloned.1.call-start = ((), (), s32[]{:S(2)}) async-start(), calls=%async_computation.10 | async-start | bytes 5898240 | tf_op jit(solution)/shard_map/reduce_scatter | solution.py:43
  33.0 56.6 %copy-start.16 = (f32[4096]{0:T(1024)}, f32[4096]{0:T(1024)S(1)}, u32[]{:S(2)}) copy-start(f32[4096]{0:T(1024)S(1)} %add_rsqrt_fusion) | copy-start | bytes 49156
  169.7 0.6 copy-start.14
  170.3 200.2 %copy-start.12 = (f32[4096]{0:T(1024)}, f32[4096]{0:T(1024)S(1)}, u32[]{:S(2)}) copy-start(f32[4096]{0:T(1024)S(1)} %fusion.77) | copy-start | bytes 49156
  246.8 58.6 %copy-start.18 = (bf16[1,1024,2560]{2,1,0:T(8,128)(2,1)S(1)}, bf16[1,1024,2560]{2,1,0:T(8,128)(2,1)}, u32[]{:S(2)}) copy-start(bf16[1,1024,2560]{2,1,0:T(8,128)(2,1)} %all-gather.19.cloned.1.call-done) | copy-start | bytes 15728644
  331.6 38.9 %copy-start.15 = (f32[4096]{0:T(1024)S(1)}, f32[4096]{0:T(1024)}, u32[]{:S(2)}) copy-start(f32[4096]{0:T(1024)} %copy-done.14) | copy-start | bytes 49156
  381.5 3.2 copy-start
  411.2 212.9 %reduce-scatter.17.cloned.1.call-start = ((), (), s32[]{:S(2)}) async-start(), calls=%async_computation.11 | async-start | bytes 5898240 | tf_op jit(solution)/shard_map/reduce_scatter | solution.py:43
  447.6 28.3 %copy-start.17 = (f32[4096]{0:T(1024)S(1)}, f32[4096]{0:T(1024)}, u32[]{:S(2)}) copy-start(f32[4096]{0:T(1024)} %copy-done.16) | copy-start | bytes 49156
  447.7 176.5 %reduce-scatter.11.cloned.1.call-start = ((), (), s32[]{:S(2)}) async-start(), calls=%async_computation.8 | async-start | bytes 5898240 | tf_op jit(solution)/shard_map/reduce_scatter | solution.py:43
  475.9 37.2 %copy-start.13 = (f32[4096]{0:T(1024)S(1)}, f32[4096]{0:T(1024)}, u32[]{:S(2)}) copy-start(f32[4096]{0:T(1024)} %copy-done.12) | copy-start | bytes 49156
  513.1 111.1 %reduce-scatter.13.cloned.1.call-start = ((), (), s32[]{:S(2)}) async-start(), calls=%async_computation.9 | async-start | bytes 5898240 | tf_op jit(solution)/shard_map/reduce_scatter | solution.py:43
  550.7 126.0 %reduce-scatter.7.cloned.1.call-start = ((), (), s32[]{:S(2)}) async-start(), calls=%async_computation.6 | async-start | bytes 5898240 | tf_op jit(solution)/shard_map/reduce_scatter | solution.py:43
  595.5 134.8 %reduce-scatter.9.cloned.1.call-start = ((), (), s32[]{:S(2)}) async-start(), calls=%async_computation.7 | async-start | bytes 5898240 | tf_op jit(solution)/shard_map/reduce_scatter | solution.py:43
  624.0 232.3 %copy-start.1 = (bf16[2,320,1024]{2,1,0:T(8,128)(2,1)S(1)}, bf16[2,320,1024]{2,1,0:T(8,128)(2,1)}, u32[]{:S(2)}) copy-start(bf16[2,320,1024]{2,1,0:T(8,128)(2,1)} %param.15) | copy-start | bytes 3932164
  624.0 208.0 %all-reduce.3.cloned.1.call-start = ((), (), s32[]{:S(2)}) async-start(), calls=%async_computation.18 | async-start | bytes 7864320 | tf_op jit(solution)/shard_map/psum | solution.py:43
  834.6 28.0 %copy-start.2 = (bf16[2,128,2560]{2,1,0:T(8,128)(2,1)S(1)}, bf16[2,128,2560]{2,1,0:T(8,128)(2,1)}, u32[]{:S(2)}) copy-start(bf16[2,128,2560]{2,1,0:T(8,128)(2,1)} %param.13) | copy-start | bytes 3932164
  834.6 28.0 %copy-start.8 = (bf16[1,128,2560]{2,1,0:T(8,128)(2,1)S(1)}, bf16[1,128,2560]{2,1,0:T(8,128)(2,1)}, u32[]{:S(2)}) copy-start(bf16[1,128,2560]{2,1,0:T(8,128)(2,1)} %get-tuple-element.9) | copy-start | bytes 1966084
  856.3 6.2 copy-start.3
  856.4 6.2 copy-start.4
  856.4 7.1 copy-start.5
  856.4 7.9 copy-start.6
  856.4 8.7 copy-start.7
  856.4 8.7 copy-start.9
  856.4 8.9 %copy-start.10 = (bf16[1,128,2560]{2,1,0:T(8,128)(2,1)S(1)}, bf16[1,128,2560]{2,1,0:T(8,128)(2,1)}, u32[]{:S(2)}) copy-start(bf16[1,128,2560]{2,1,0:T(8,128)(2,1)} %get-tuple-element.11) | copy-start | bytes 1966084
  856.4 9.1 %copy-start.11 = (bf16[1,128,2560]{2,1,0:T(8,128)(2,1)S(1)}, bf16[1,128,2560]{2,1,0:T(8,128)(2,1)}, u32[]{:S(2)}) copy-start(bf16[1,128,2560]{2,1,0:T(8,128)(2,1)} %get-tuple-element.12) | copy-start | bytes 1966084
Sparse Core Ops, SparseCore 0:
  10.4 39.7 all-gather.12
  52.6 36.9 all-gather.14
  92.0 36.9 all-gather.16
  131.3 36.9 all-gather.20
  170.5 36.9 all-gather.22
  209.8 36.9 all-gather.18
  411.4 50.3 reduce-scatter.14
  465.1 50.3 reduce-scatter.16
  518.9 50.3 reduce-scatter.10
  572.5 50.3 reduce-scatter.12
  626.3 50.3 reduce-scatter.6
  679.9 50.3 reduce-scatter.8
  733.0 98.9 all-reduce.2
where the time goes:
time: 886 us; the launch traced here: 879 us
  matrix products  531 us (60%)
  waiting for transfers between devices  243 us (27%)
  local copies, waits for them, and re-layouts  37.1 us (4%)
  other arithmetic  36.2 us (4%)
  between operations  17.2 us (2%)
  blocking collectives  13.8 us (2%)
    dot_general x5, matrix products, layer(): up = jnp.dot(a, w['w_up'], preferred_element_type=jnp.float32)  194 us
    dot_general x5, matrix products, layer(): gate = jnp.dot(a, w['w_gate'], preferred_element_type=jnp.float32)  188 us
    dot_general x5, matrix products, matmul(): jnp.dot(a, w, preferred_element_type=jnp.float32).astype(jnp.bfloat16)  150 us
    reduce_scatter x6, waiting for transfers between devices, summed(): lax.psum_scatter(term, 's', scatter_dimension=0, tiled=True)  106 us
    psum x1, waiting for transfers between devices, summed(): lax.psum(lax.psum_scatter(term, 's', scatter_dimension=0, tiled=True), 'r')  102 us
    all_gather x6, waiting for transfers between devices, fetched(): lax.all_gather(w[number], 's', axis=0, tiled=True)  33 us
    unnamed x40, local copies, waits for them, and re-layouts  29.8 us
  transfers between devices with their start and end apart: 13, of which 7 were waited for; matrix products, arithmetic and copies ran while one was open for 47% of the time, Pallas kernels for 0%

commit v1 on v0

v1 whole, which is shorter than its diff:
```python
import functools

import jax
import jax.numpy as jnp
from jax import lax
from jax.experimental import pallas as pl
from jax.experimental.pallas import tpu as pltpu
from jax.sharding import PartitionSpec as P

BF, F32 = jnp.bfloat16, jnp.float32
T, D, FF = 4096, 1024, 2560
NJ, FB = 5, 512
TT = 1024
LAST = T // TT - 1
VMEM_LIMIT = 63 * 1024 * 1024
NN = (((1,), (0,)), ((), ()))
NT = (((1,), (1,)), ((), ()))


def dot(a, b, dims=NN):
    return lax.dot_general(a, b, dims, preferred_element_type=F32)


def call(kernel, flops, nbytes, **kw):
    return pl.pallas_call(
        kernel,
        cost_estimate=pl.CostEstimate(flops=int(flops), bytes_accessed=int(nbytes), transcendentals=0),
        compiler_params=pltpu.CompilerParams(vmem_limit_bytes=VMEM_LIMIT),
        **kw,
    )


def norm_scale(wide):
    return lax.rsqrt(jnp.mean(wide * wide, -1, keepdims=True) + 1e-6)


def flip(me, k):
    out = me
    for bit in (1, 2, 4):
        if k & bit:
            out = out + bit - 2 * bit * lax.rem(lax.div(out, bit), 2)
    return out


def forward_kernel(
    x_ref, dy_ref, wg_hbm, wu_hbm, wd_hbm, at_ref, dyt_ref, g_ref, u_ref, hid_ref, wd_full, a_all, wg, wu, sems, rsems, own_sems
):
    me = lax.axis_index("s")
    j, t = pl.program_id(0), pl.program_id(1)

    def copies(c, m):
        first, second = ((4, 2), (2, 4))[m]

        def part(ref, k, whole):
            if c is None:
                return ref.at[pl.ds(0 if whole else pl.multiple_of(flip(me, k) * 320, 64), 320), pl.ds(512 * m, 512)]
            return ref.at[pl.ds(0 if whole else pl.multiple_of(flip(me, k) * 128, 128), 128), pl.ds(pl.multiple_of(c * FB, FB), FB)]

        full = wd_full if c is None else (wg, wu)[m]
        mine = wd_hbm.at[0] if c is None else (wg_hbm, wu_hbm)[m].at[0]
        n = NJ if c is None else c

        def copy(i, k, to):
            src = part(mine, 0, True) if k == 0 else part(full, k, False)
            return lambda: pltpu.make_async_remote_copy(
                src_ref=src, dst_ref=part(full, k, False), send_sem=sems.at[n, m, i], recv_sem=rsems.at[n, m, i],
                device_id={"s": flip(me, to)}, device_id_type=pl.DeviceIdType.MESH,
            )

        direct = [copy(0, 0, first), copy(1, 0, second), copy(2, 0, 1)]
        forward = [copy(3, first, second)]
        core = [copy(4, first, 1), copy(5, second, 1)], [copy(6, 6, 1)]
        return direct, forward, core

    def each(c, do):
        for m in range(2):
            do(*copies(c, m))

    def starts(cs):
        for x in cs:
            x().start()

    def begin(c):
        each(c, lambda direct, forward, core: starts(direct))

    def onward(c):
        def do(direct, forward, core):
            for x in direct[:2]:
                x().wait_recv()
            starts(forward)
            starts(core[0])

        each(c, do)

    def across(c):
        def do(direct, forward, core):
            forward[0]().wait_recv()
            starts(core[1])

        each(c, do)

    def here(c):
        def do(direct, forward, core):
            for x in direct[2:] + core[0] + core[1]:
                x().wait_recv()

        each(c, do)

    def sent(c):
        def do(direct, forward, core):
            for x in direct + forward + core[0] + core[1]:
                x().wait_send()

        each(c, do)

    def own():
        rows = pl.ds(pl.multiple_of(me * 128, 128), 128)
        down_rows = pl.ds(pl.multiple_of(me * 320, 64), 320)
        return [
            lambda: pltpu.make_async_copy(wg_hbm.at[0], wg.at[rows], own_sems.at[0]),
            lambda: pltpu.make_async_copy(wu_hbm.at[0], wu.at[rows], own_sems.at[1]),
            lambda: pltpu.make_async_copy(wd_hbm.at[0], wd_full.at[down_rows], own_sems.at[2]),
        ]

    @pl.when((j == 0) & (t == 0))
    def _():
        barrier = pltpu.get_barrier_semaphore()
        for k in (1, 2, 4):
            pl.semaphore_signal(barrier, inc=1, device_id={"s": flip(me, k)}, device_id_type=pl.DeviceIdType.MESH)
        pl.semaphore_wait(barrier, 3)
        begin(0)
        starts(own())

    @pl.when(j == 0)
    def _():
        wide = x_ref[...].astype(F32)
        a = (wide * norm_scale(wide)).astype(BF)
        a_all[pl.ds(pl.multiple_of(t * TT, TT), TT), :] = a
        at_ref[...] = a.T
        dyt_ref[...] = dy_ref[...].T

    @pl.when(((j == 0) & (t == 2)) | ((j > 0) & (j < NJ) & (t == 0)))
    def _():
        onward(j)

        @pl.when(j < NJ - 1)
        def _():
            begin(j + 1)

        @pl.when(j == NJ - 1)
        def _():
            begin(None)

    @pl.when(((j == 0) & (t == LAST)) | ((j > 0) & (j < NJ) & (t == 2)))
    def _():
        across(j)

    @pl.when((j < NJ) & (t == LAST))
    def _():
        here(j)

    @pl.when((j == 0) & (t == LAST))
    def _():
        for x in own():
            x().wait()

    @pl.when((j == NJ) & (t == 1))
    def _():
        onward(None)

    @pl.when(j > 0)
    def _():
        a = a_all[pl.ds(pl.multiple_of(t * TT, TT), TT), :]
        cols = pl.ds(pl.multiple_of((j - 1) * FB, FB), FB)
        g = dot(a, wg[:, cols])
        u = dot(a, wu[:, cols])
        g_ref[...] = g
        u_ref[...] = u
        hid_ref[...] = (g * jax.nn.sigmoid(g) * u).astype(BF)

    @pl.when((j == NJ) & (t == LAST))
    def _():
        across(None)
        here(None)
        sent(None)
        lax.fori_loop(0, NJ, lambda c, _: (sent(c), 0)[1], 0)


def forward(x, dy, wg, wu, wd):
    rows = pl.BlockSpec((TT, D), lambda j, t: (jnp.where(j == 0, t, LAST), 0))
    cols = pl.BlockSpec((D, TT), lambda j, t: (0, jnp.where(j == 0, t, LAST)))
    tile = pl.BlockSpec((TT, FB), lambda j, t: (jnp.where(j == 0, 0, t), jnp.maximum(j - 1, 0)))
    anywhere = pl.BlockSpec(memory_space=pl.ANY)
    sems = pltpu.SemaphoreType.DMA((NJ + 1, 2, 7))
    return pl.pallas_call(
        forward_kernel,
        cost_estimate=pl.CostEstimate(flops=4 * T * D * FF, bytes_accessed=10 * T * FF, transcendentals=0),
        compiler_params=pltpu.CompilerParams(vmem_limit_bytes=VMEM_LIMIT, collective_id=3, has_side_effects=True),
        name="forward", grid=(NJ + 1, T // TT),
        in_specs=[rows, rows] + [anywhere] * 3, out_specs=[cols, cols, tile, tile, tile, anywhere],
        out_shape=[
            jax.ShapeDtypeStruct((D, T), BF), jax.ShapeDtypeStruct((D, T), BF), jax.ShapeDtypeStruct((T, FF), F32),
            jax.ShapeDtypeStruct((T, FF), F32), jax.ShapeDtypeStruct((T, FF), BF), jax.ShapeDtypeStruct((FF, D), BF),
        ],
        scratch_shapes=[
            pltpu.VMEM((T, D), BF), pltpu.VMEM((D, FF), BF), pltpu.VMEM((D, FF), BF), sems, sems, pltpu.SemaphoreType.DMA((3,)),
        ],
    )(x, dy, wg, wu, wd)


def down_kernel(hid_ref, x_ref, wd_ref, h_ref, a_ref, at_ref):
    h = x_ref[...] + dot(hid_ref[...], wd_ref[...]).astype(BF)
    h_ref[...] = h
    wide = h.astype(F32)
    a = (wide * norm_scale(wide)).astype(BF)
    a_ref[...] = a
    at_ref[...] = a.T


def down(hid, x, wd):
    rows = pl.BlockSpec((512, D), lambda t: (t, 0))
    return call(
        down_kernel, 2 * T * D * FF, 2 * T * FF + 8 * T * D, name="down", grid=(T // 512,),
        in_specs=[pl.BlockSpec((512, FF), lambda t: (t, 0)), rows, pl.BlockSpec((FF, D), lambda t: (0, 0))],
        out_specs=[rows, rows, pl.BlockSpec((D, 512), lambda t: (0, t))],
        out_shape=[jax.ShapeDtypeStruct((T, D), BF), jax.ShapeDtypeStruct((T, D), BF), jax.ShapeDtypeStruct((D, T), BF)],
    )(hid, x, wd)


def cat(refs):
    return jnp.concatenate([r[...] for r in refs], axis=1)


def comm_scratch(chunks):
    blocks = (2, 2, 384, 512)
    return [
        pltpu.VMEM(blocks, F32),
        pltpu.VMEM(blocks, BF),
        pltpu.VMEM((2, *blocks), BF),
        pltpu.VMEM((2, 2, 192, 512), BF),
        pltpu.VMEM((2, 2, 2, 192, 512), BF),
        pltpu.VMEM((2, 192, 512), BF),
        pltpu.VMEM((2, 2, 192, 512), BF),
        pltpu.VMEM((384, 512), BF),
        pltpu.VMEM((2, 384, 512), BF),
        pltpu.SemaphoreType.DMA((6,)),
        pltpu.SemaphoreType.DMA((6, 2)),
    ]


def exchange(me, peer, keep, send1, recv1, send2, recv2, send3, recv3, send4, recv4, sems, rsems, out_ref):
    one, two, four = ({"s": flip(me, k)} for k in (1, 2, 4))
    z = {"r": peer}

    def copy(i, src, dst, slot, to):
        return pltpu.make_async_remote_copy(
            src_ref=src, dst_ref=dst, send_sem=sems.at[i], recv_sem=rsems.at[i, slot], device_id=to, device_id_type=pl.DeviceIdType.MESH
        )

    def c1(slot):
        return [copy(0, send1, recv1.at[slot], slot, one)]

    def c2(slot):
        return [copy(1 + i, send2.at[i], recv2.at[slot, i], slot, to) for i, to in enumerate((four, two))]

    def c3(slot):
        return [copy(3 + i, send3.at[i], recv3.at[slot, i], slot, to) for i, to in enumerate((two, four))]

    def c4(slot):
        return [copy(5, send4, recv4.at[slot], slot, z)]

    def start(cs):
        for c in cs:
            c.start()

    def wait(cs):
        for c in cs:
            c.wait()

    lo, hi = slice(0, 192), slice(192, 384)

    def s1(slot):
        start(c1(slot))

    def s2(slot):
        wait(c1(slot))
        for k in range(2):
            def total(kx, ky, rows):
                return keep[kx, ky, rows] + recv1[slot, kx, ky, rows].astype(F32)

            send2[0, k] = total(1, k, lo).astype(BF)
            send2[1, k] = total(k, 1, hi).astype(BF)
            keep[0, k, lo] = total(0, k, lo)
            keep[k, 0, hi] = total(k, 0, hi)
        start(c2(slot))

    def s3(slot):
        wait(c2(slot))
        send3[0] = (keep[0, 1, lo] + recv2[slot, 0, 1].astype(F32)).astype(BF)
        send3[1] = (keep[1, 0, hi] + recv2[slot, 1, 1].astype(F32)).astype(BF)
        keep[0, 0, lo] = keep[0, 0, lo] + recv2[slot, 0, 0].astype(F32)
        keep[0, 0, hi] = keep[0, 0, hi] + recv2[slot, 1, 0].astype(F32)
        start(c3(slot))

    def s4(slot):
        wait(c3(slot))
        send4[lo] = (keep[0, 0, lo] + recv3[slot, 0].astype(F32)).astype(BF)
        send4[hi] = (keep[0, 0, hi] + recv3[slot, 1].astype(F32)).astype(BF)
        start(c4(slot))

    def final(e, slot):
        wait(c4(slot))
        out_ref[e] = (send4[...].astype(F32) + recv4[slot].astype(F32)).astype(BF)

    return s1, s2, s3, s4, final


def grads_kernel(second, *refs):
    if second:
        a_ref, *refs = refs
        wg, wu, refs = refs[:4], refs[4:8], refs[8:]
        dy_ref, at_ref, dyt_ref, wd_ref, out_ref, dg_ref, du_ref, hkeep, hsend, accg, accu, accd, down_ref, hsems, *comm = refs
    else:
        g_refs, u_refs, refs = refs[:4], refs[4:8], refs[8:]
        dy_ref, at_ref, dyt_ref, wd_ref, hkeep, hsend, out_ref, accg, accu, accd, down_ref, hsems, *comm = refs
    keep, send1 = comm[:2]
    me, group = lax.axis_index("s"), lax.axis_index("r")
    j, t = pl.program_id(0), pl.program_id(1)
    last = pl.num_programs(1) - 1
    off = 0 if second else 1
    s1, s2, s3, s4, final = exchange(me, 1 - group, *comm, out_ref)

    @pl.when((j == 0) & (t == 0))
    def _():
        barrier = pltpu.get_barrier_semaphore()
        for to in [{"s": flip(me, k)} for k in (1, 2, 4)] + [{"r": 1 - group}]:
            pl.semaphore_signal(barrier, inc=1, device_id=to, device_id_type=pl.DeviceIdType.MESH)
        pl.semaphore_wait(barrier, 4)
        if not second:
            hands = [pltpu.make_async_copy(hkeep, keep, hsems.at[0]), pltpu.make_async_copy(hsend, send1, hsems.at[1])]
            for h in hands:
                h.start()
            for h in hands:
                h.wait()
            s1(0)

    @pl.when(t == 0)
    def _():
        for acc in (accg, accu, accd):
            acc[...] = jnp.zeros_like(acc)

    def front(i):
        two = slice(2 * i, 2 * i + 2)
        cols = slice(256 * i, 256 * (i + 1))
        if second:
            a = a_ref[...]
            g, u = dot(a, cat(wg[two])), dot(a, cat(wu[two]))
        else:
            g, u = cat(g_refs[two]), cat(u_refs[two])
        dh = dot(dy_ref[...], wd_ref[two].reshape(256, D), NT).astype(BF).astype(F32)
        s = jax.nn.sigmoid(g)
        silu = g * s
        hid = (silu * u).astype(BF)
        du = (dh * silu).astype(BF)
        dg = (dh * u * (s + silu * (1.0 - s))).astype(BF)
        if second:
            dg_ref[:, cols] = dg
            du_ref[:, cols] = du
        return hid, dg, du

    def back(i, hid, dg, du):
        cols = slice(256 * i, 256 * (i + 1))
        accg[:, cols] += dot(at_ref[...], dg)
        accu[:, cols] += dot(at_ref[...], du)
        accd[:, cols] += dot(dyt_ref[...], hid)

    zero, one = front(0), front(1)
    back(0, *zero)
    back(1, *one)

    e = j - 1 + off
    slot = lax.rem(e + 2, 2)
    for at_t, stage in ((0, s2), (2, s3), (3, s4)):
        @pl.when((t == at_t) & (e >= 0))
        def _():
            stage(slot)

    @pl.when((t == 1) & (e >= 1))
    def _():
        final(e - 1, lax.rem(e + 1, 2))

    @pl.when(t == last)
    def _():
        down_ref[...] = accd[...].T
        for k in range(8):
            out = (keep, send1)[k % 2]
            kx, ky = k // 4, k // 2 % 2
            d = flip(me, k)
            wide = pl.ds(pl.multiple_of(d * 128, 128), 128)
            rows = pl.ds(pl.multiple_of(d * 64, 64), 64)
            out[kx, ky, 0:128] = accg[wide, :].astype(out.dtype)
            out[kx, ky, 128:256] = accu[wide, :].astype(out.dtype)
            out[kx, ky, 256:320] = down_ref[rows, 0:512].astype(out.dtype)
            out[kx, ky, 320:384] = down_ref[rows, 512:1024].astype(out.dtype)

    new = lax.rem(e + 3, 2)
    end = (t == last) & (j == NJ - 1)
    if second:
        @pl.when((t == last) & (j < NJ - 1))
        def _():
            s1(new)

        @pl.when(end)
        def _():
            hands = [pltpu.make_async_copy(keep, hkeep, hsems.at[0]), pltpu.make_async_copy(send1, hsend, hsems.at[1])]
            for h in hands:
                h.start()
            final(NJ - 2, (NJ - 2) % 2)
            for h in hands:
                h.wait()
    else:
        @pl.when(t == last)
        def _():
            s1(new)

        @pl.when(end)
        def _():
            final(NJ - 1, (NJ - 1) % 2)
            for stage in (s2, s3, s4):
                stage(NJ % 2)
            final(NJ, NJ % 2)


def grads(gate_up_of, dy, at, dyt, wd, handed=None):
    second = handed is None
    rows = pl.BlockSpec((TT, D), lambda j, t: (t, 0))
    cols = pl.BlockSpec((D, TT), lambda j, t: (0, t))
    if second:
        a, wg, wu = gate_up_of
        wspec = [pl.BlockSpec((D, 128), lambda j, t, c=c: (0, 5 * c + j)) for c in range(4)]
        ops, specs = [a] + [wg] * 4 + [wu] * 4, [rows] + wspec * 2
    else:
        g, u = gate_up_of
        gspec = [pl.BlockSpec((TT, 128), lambda j, t, c=c: (t, 5 * c + j)) for c in range(4)]
        ops, specs = [g] * 4 + [u] * 4, gspec * 2
    chunks = NJ - 1 if second else NJ + 1
    ops += [dy, at, dyt, wd.reshape(4, NJ, 128, D)]
    specs += [rows, cols, cols, pl.BlockSpec((4, 1, 128, D), lambda j, t: (0, j, 0, 0))]
    outs = [jax.ShapeDtypeStruct((chunks, 384, 512), BF)]
    ospecs = [pl.BlockSpec((chunks, 384, 512), lambda j, t: (0, 0, 0))]
    hand = [jax.ShapeDtypeStruct((2, 2, 384, 512), F32), jax.ShapeDtypeStruct((2, 2, 384, 512), BF)]
    anywhere = [pl.BlockSpec(memory_space=pl.ANY)] * 2
    if second:
        outs += [jax.ShapeDtypeStruct((T, FF), BF)] * 2 + hand
        ospecs += [pl.BlockSpec((TT, FB), lambda j, t: (t, j))] * 2 + anywhere
    else:
        ops += handed
        specs += anywhere
    return pl.pallas_call(
        functools.partial(grads_kernel, second),
        cost_estimate=pl.CostEstimate(flops=(12 if second else 8) * T * D * FF, bytes_accessed=40 * T * D * NJ, transcendentals=0),
        compiler_params=pltpu.CompilerParams(vmem_limit_bytes=VMEM_LIMIT, collective_id=1 if second else 2, has_side_effects=True),
        name="grads_second" if second else "grads_first", grid=(NJ, T // TT),
        in_specs=specs, out_specs=ospecs, out_shape=outs,
        scratch_shapes=[pltpu.VMEM((D, FB), F32)] * 3 + [pltpu.VMEM((FB, D), F32), pltpu.SemaphoreType.DMA((2,))] + comm_scratch(chunks),
    )(*ops)


def dstate_kernel(groups, *refs):
    n = len(groups)
    dgs, dus, (h_ref, dy_ref, wg_ref, wu_ref, dh_ref, dht_ref) = refs[:n], refs[n : 2 * n], refs[2 * n :]

    def back(parts, w_ref):
        total, j = None, 0
        for ref, count in zip(parts, groups, strict=True):
            for k in range(count):
                w = jnp.concatenate([w_ref[:, 128 * (5 * c + j) : 128 * (5 * c + j + 1)] for c in range(4)], axis=1)
                one = dot(ref[:, FB * k : FB * (k + 1)], w, NT)
                total = one if total is None else total + one
                j += 1
        return total.astype(BF)

    da = (back(dgs, wg_ref) + back(dus, wu_ref)).astype(F32)
    wide = h_ref[...].astype(F32)
    scale = norm_scale(wide)
    along = jnp.sum(da * wide, -1, keepdims=True)
    dn = (da * scale - wide * (along * scale * scale * scale * (1.0 / D))).astype(BF)
    dh = dy_ref[...] + dn
    dh_ref[...] = dh
    dht_ref[...] = dh.T


def dstate(dgs, dus, h, dy, wg, wu):
    groups = tuple(d.shape[1] // FB for d in dgs)
    tt = 512
    rows = pl.BlockSpec((tt, D), lambda t: (t, 0))
    wide = [pl.BlockSpec((tt, FB * n), lambda t: (t, 0)) for n in groups]
    w = pl.BlockSpec((D, FF), lambda t: (0, 0))
    return call(
        functools.partial(dstate_kernel, groups), 4 * T * D * FF, 4 * T * FF + 8 * T * D, name="dstate", grid=(T // tt,),
        in_specs=wide * 2 + [rows, rows, w, w],
        out_specs=[rows, pl.BlockSpec((D, tt), lambda t: (0, t))],
        out_shape=[jax.ShapeDtypeStruct((T, D), BF), jax.ShapeDtypeStruct((D, T), BF)],
    )(*dgs, *dus, h, dy, wg, wu)


def adamw(w, m, v, g):
    m = 0.9 * m + 0.1 * g
    v = 0.95 * v + 0.05 * g * g
    step = m * lax.rsqrt(v + 1e-8) + 0.1 * w
    return (w - 0.02 * step).astype(BF), m, v


def solution(mesh):
    size = mesh.shape["s"]

    def swap(v, k):
        return lax.ppermute(v, "s", [(i, i ^ k) for i in range(size)])

    def gradients_of(parts):
        whole = jnp.concatenate(parts, axis=0)
        gate, up = (
            whole[:, 128 * i : 128 * (i + 1)].reshape(NJ, 128, 4, 128).transpose(1, 2, 0, 3).reshape(128, FF) for i in range(2)
        )
        rows = jnp.concatenate([whole[:, 256:320], whole[:, 320:384]], axis=2)
        core = lax.axis_index("s") % 2
        mine = jnp.where(core == 0, rows[:3], rows[2:])
        other = swap(jnp.where(core == 0, rows[3:], rows[:2]), 1)
        units = jnp.stack([mine[0], other[0], mine[1], other[1], mine[2]])
        return gate, up, units.reshape(320, D)

    def fetched(weights, number):
        return [lax.all_gather(w[number], "s", axis=0, tiled=True) for w in weights]

    def step(x, dy, *arrays):
        weights, m, v = (arrays[i : i + 3] for i in (0, 3, 6))
        x, dy = x[0], dy[0]
        wg1, wu1, wd1 = fetched(weights, 1)
        a0t, dyt, g0, u0, hid0, wd0 = forward(x, dy, *weights)
        h1, a1, a1t = down(hid0, x, wd0)
        done1, dg, du, *handed = grads((a1, wg1, wu1), dy, a1t, dyt, wd1)
        dh1, dh1t = dstate([dg], [du], h1, dy, wg1, wu1)
        done0, = grads((g0, u0), dh1, a0t, dh1t, wd0, handed)
        parts1, parts0 = [done1, done0[:1]], [done0[1:]]
        both = [gradients_of(parts0), gradients_of(parts1)]
        gs = [[both[l][i].astype(F32) for l in range(2)] for i in range(3)]
        squares = lax.psum(sum(jnp.sum(g * g) for pair in gs for g in pair), "s")
        factor = jnp.minimum(1.0, 0.5 * lax.rsqrt(squares / (3 * 2 * D * FF) + 1e-30))
        new = [
            adamw(w.astype(F32), mm, vv, jnp.stack(g) * factor) for w, mm, vv, g in zip(weights, m, v, gs, strict=True)
        ]
        return tuple(one[which] for which in range(3) for one in new)

    states, cut = P(("rep", "r", "s"), None, None), P(None, "s", None)
    return jax.shard_map(
        step, mesh=mesh, in_specs=(states, states) + (cut,) * 9, out_specs=(P("rep", "s", None),) * 9, check_vma=False,
    )
```

time: 886 us -> 644 us (0.73)
  matrix products: 531 us -> 0 us
  Pallas kernels: 0 us -> 531 us
  waiting for transfers between devices: 243 us -> 0.08 us
  local copies, waits for them, and re-layouts: 37.1 us -> 57 us
  other arithmetic: 36.2 us -> 22.4 us
    pallas_call x0 -> x5, Pallas kernels: none -> 531 us  [the longest x2 318 us: grads(): pl.pallas_call(functools.partial(grads_kernel, second), cost_estimate=pl....]
    dot_general x15 -> x0, matrix products: 531 us -> none  [the longest x5 194 us: layer(): up = jnp.dot(a, w['w_up'], preferred_element_type=jnp.float32)]
    reduce_scatter x6 -> x0, waiting for transfers between devices: 106 us -> none  [summed(): lax.psum_scatter(term, 's', scatter_dimension=0, tiled=True)]
    psum x1 -> x0, waiting for transfers between devices: 102 us -> none  [summed(): lax.psum(lax.psum_scatter(term, 's', scatter_dimension=0, tiled=True), 'r')]
    all_gather x6 -> x3, waiting for transfers between devices: 33 us -> 0.02 us  [fetched(): return [lax.all_gather(w[number], 's', axis=0, tiled=True) for w in weights]]
    add_any x1 -> x0, other arithmetic: 10.9 us -> none  [normed(): wide = h.astype(jnp.float32)]
    convert_element_type x0 -> x8, local copies, waits for them, and re-layouts: none -> 9.54 us  [step(): gs = [[both[l][i].astype(F32) for l in range(2)] for i in range(3)]]
    unnamed x40 -> x48, local copies, waits for them, and re-layouts: 29.8 us -> 37.1 us
  transfers between devices with their start and end apart: 13 -> 5, of which waited for: 7 -> 0; matrix products, arithmetic and copies ran while one was open for 47% -> 5% of each run, Pallas kernels for 0% -> 24%
where the time goes in v1:
time: 644 us; the launch traced here: 643 us
  Pallas kernels  531 us (82%)
  local copies, waits for them, and re-layouts  57 us (9%)
  other arithmetic  22.4 us (3%)
  between operations  18.6 us (3%)
  blocking collectives  13.3 us (2%)
    pallas_call x2, Pallas kernels, grads(): pl.pallas_call(functools.partial(grads_kernel, second), cost_estimate=pl....  318 us
    pallas_call x1, Pallas kernels, forward(): pl.pallas_call(forward_kernel, cost_estimate=pl.CostEstimate(flops=4 * T...  121 us
    pallas_call x1, Pallas kernels, dstate(): call(functools.partial(dstate_kernel, groups), 4 * T * D * FF, 4 * T * FF...  59.3 us
    unnamed x48, local copies, waits for them, and re-layouts  37.1 us
    pallas_call x1, Pallas kernels, down(): call(down_kernel, 2 * T * D * FF, 2 * T * FF + 8 * T * D, name='down', gr...  32.7 us
    convert_element_type x3, other arithmetic, adamw(): return ((w - 0.02 * step).astype(BF), m, v)  15.7 us
    psum x1, blocking collectives, step(): squares = lax.psum(sum((jnp.sum(g * g) for pair in gs for g in pair)), 's')  13.3 us
  transfers between devices with their start and end apart: 5, of which 0 were waited for; matrix products, arithmetic and copies ran while one was open for 5% of the time, Pallas kernels for 24%

profile of v1, /device:TPU:0, one launch (start us, length us, event | category | flops | bytes accessed | tf_op | source)
XLA Modules:
  0.0 643.5 jit_solution(4529558714724978736)
XLA Ops:
  7.2 2.0 slice.95
  9.3 2.1 slice.96
  11.4 2.1 slice.97
  13.5 1.4 copy.29
  14.9 1.4 copy.24
  16.4 3.4 copy.30
  19.7 2.1 copy.33
  21.8 3.4 copy.25
  25.2 2.1 copy.28
  27.3 121.2 %forward.1 = (bf16[1024,4096]{1,0:T(8,128)(2,1)}, bf16[1024,4096]{1,0:T(8,128)(2,1)}, f32[4096,2560]{1,0:T(8,128)}, f32[4096,2560]{1,0:T(8,128)}, bf16[4096,2560...) custom-call(bf16[4096,1024]{1,0:T(8,128)(2,1)} %bitcast.27, bf16[4096,1024]{1,0:T(8,128)(2,1)} %bitcast.29, ...), custom_call_target="tpu_custom_call" | custom-call | flops 42949672960 | bytes 104857600 | tf_op jit(solution)/shard_map/forward/pallas_call | solution.py:195
  148.4 32.7 %down.1 = (bf16[4096,1024]{1,0:T(8,128)(2,1)}, bf16[4096,1024]{1,0:T(8,128)(2,1)}, bf16[1024,4096]{1,0:T(8,128)(2,1)}) custom-call(bf16[4096,2560]{1,0:T(8,128)(2,1)} %get-tuple-element.27.hid_ref, bf16[4096,1024]{1,0:T(8,128)(2,1)} %bitcast.28, bf16[2560,1024]{1,0:T(8,128)(2,1)} %get-tuple-element.28.wd_ref), custom_call_target="tpu_custom_call" | custom-call | flops 21474836480 | bytes 54525952 | tf_op jit(solution)/shard_map/down/pallas_call | solution.py:222
  181.1 170.0 %grads_second.1 = (bf16[4,384,512]{2,1,0:T(8,128)(2,1)}, bf16[4096,2560]{1,0:T(8,128)(2,1)}, bf16[4096,2560]{1,0:T(8,128)(2,1)}, f32[2,2,384,512]{3,2,1,0:T(8,128)}, bf16[2,2,384,512]{3,2,1,0:T(8,128)(2,1)}) custom-call(bf16[4096,1024]{1,0:T(8,128)(2,1)} %get-tuple-element.29.refs_0_, bf16[1024,2560]{1,0:T(8,128)(2,1)} %bitcast.32, ...), custom_call_target="tpu_custom_call" | custom-call | flops 128849018880 | bytes 838860800 | tf_op jit(solution)/shard_map/grads_second/pallas_call | solution.py:459
  351.2 59.3 %dstate.1 = (bf16[4096,1024]{1,0:T(8,128)(2,1)}, bf16[1024,4096]{1,0:T(8,128)(2,1)}) custom-call(bf16[4096,2560]{1,0:T(8,128)(2,1)} %get-tuple-element.32.refs_0_, bf16[4096,2560]{1,0:T(8,128)(2,1)} %get-tuple-element.33.refs_1_, bf16[4096,1024]{1,0:T(8,128)(2,1)} %get-tuple-element.34.refs_2_, bf16[4096,1024]{1,0:T(8,128)(2,1)} %bitcast.31, ...), custom_call_target="tpu_custom_call" | custom-call | flops 42949672960 | bytes 75497472 | tf_op jit(solution)/shard_map/dstate/pallas_call | solution.py:499
  410.5 148.3 %grads_first.1 = bf16[6,384,512]{2,1,0:T(8,128)(2,1)} custom-call(f32[4096,2560]{1,0:T(8,128)} %get-tuple-element.25.refs_0_.refs_1_.refs_2_.refs_3_, f32[4096,2560]{1,0:T(8,128)} %get-tuple-element.25.refs_0_.refs_1_.refs_2_.refs_3_, f32[4096,2560]{1,0:T(8,128)} %get-tuple-element.25.refs_0_.refs_1_.refs_2_.refs_3_, ...), custom_call_target="tpu_custom_call" | custom-call | flops 85899345920 | bytes 838860800 | tf_op jit(solution)/shard_map/grads_first/pallas_call | solution.py:459
  558.8 1.1 slice.99
  560.0 1.1 fusion.27
  561.1 1.8 multiply_reduce_fusion.2
  566.6 1.6 convert_element_type.152
  568.2 1.5 copy.32
  569.9 1.5 copy.31
  571.5 1.5 copy.27
  589.0 2.2 copy.26
  591.1 13.3 %psum.7 = f32[]{:T(128)} all-reduce(f32[]{:T(128)S(6)} %add.69), channel_id=1, replica_groups=mesh['rep'=1,'r'=2,'s'=8] {'s'}, use_global_device_ids=true, to_apply=%region_6.7 | all-reduce | flops 1 | bytes 8 | tf_op jit(solution)/shard_map/psum | solution.py:547
  605.2 5.3 fusion.5
  610.4 3.4 copy.37
  613.8 2.1 copy.39
  615.9 2.6 copy.35
  618.4 5.2 fusion.2
  623.7 3.4 copy.36
  627.0 2.1 copy.38
  629.1 2.6 copy.34
  631.7 5.2 fusion.8
  (63 shorter events, 16.2 us)
Async XLA Ops:
  7.2 173.9 %all-gather.7.cloned.1.call-start = ((), (), s32[]{:S(2)}) async-start(), calls=%async_computation | async-start | bytes 5898240 | tf_op jit(solution)/shard_map/all_gather | solution.py:533
  9.2 4.3 copy-start.9
  9.2 171.9 %all-gather.9.cloned.1.call-start = ((), (), s32[]{:S(2)}) async-start(), calls=%async_computation.1 | async-start | bytes 5898240 | tf_op jit(solution)/shard_map/all_gather | solution.py:533
  11.3 3.6 copy-start.8
  11.4 169.8 %all-gather.11.cloned.1.call-start = ((), (), s32[]{:S(2)}) async-start(), calls=%async_computation.2 | async-start | bytes 5898240 | tf_op jit(solution)/shard_map/all_gather | solution.py:533
  16.4 3.4 copy-start.11
  21.8 3.4 copy-start.12
  558.8 2.3 copy-start.1
  561.1 1.9 copy-start
  565.9 0.7 copy-start.13
  565.9 11.7 %collective-permute-start.1 = (bf16[2,64,1024]{2,1,0:T(8,128)(2,1)}, bf16[2,64,1024]{2,1,0:T(8,128)(2,1)}, u32[]{:S(2)}, u32[]{:S(2)}) collective-permute-start(bf16[2,64,1024]{2,1,0:T(8,128)(2,1)} %slice_select_fusion.1), channel_id=1, source_target_pairs={{0,1},{1,0},{2,3},{3,2},{4,5},{5,4},{6,7},{7,6},{8,9},{9,8},{10,11... | collective-permute-start | bytes 786440 | tf_op jit(solution)/shard_map/ppermute | solution.py:518
  566.0 16.3 %collective-permute-start = (bf16[2,64,1024]{2,1,0:T(8,128)(2,1)S(1)}, bf16[2,64,1024]{2,1,0:T(8,128)(2,1)}, u32[]{:S(2)}, u32[]{:S(2)}) collective-permute-start(bf16[2,64,1024]{2,1,0:T(8,128)(2,1)S(1)} %fusion.20), channel_id=1, source_target_pairs={{0,1},{1,0},{2,3},{3,2},{4,5},{5,4},{6,7},{7,6},{8,9},{9,8},{10,11... | collective-permute-start | bytes 786440 | tf_op jit(solution)/shard_map/ppermute | solution.py:518
  574.0 31.1 %copy-start.3 = (f32[2,128,2560]{1,2,0:T(8,128)S(1)}, f32[2,128,2560]{1,2,0:T(8,128)}, u32[]{:S(2)}) copy-start(f32[2,128,2560]{1,2,0:T(8,128)} %copy.30) | copy-start | bytes 7864324
  585.9 0.8 copy-start.6
  610.4 3.4 copy-start.4
  615.9 2.6 copy-start.2
  623.7 3.4 copy-start.5
  629.1 2.6 copy-start.7
  629.1 2.6 copy-start.10
Sparse Core Ops, SparseCore 0:
  10.4 53.9 all-gather.6
  66.8 56.5 all-gather.8
  125.8 40.2 all-gather.10

commit v2 on v1

--- a/solution.py
+++ b/solution.py
@@ -42,94 +42,112 @@
     return out
 
 
+def block(ref, rows, first, cols):
+    return ref.at[pl.ds(rows, first), cols]
+
+
+class Gather:
+    def __init__(self, me, mine, full, order, sems, rsems):
+        first, second = order
+
+        def copy(i, k, to):
+            return lambda: pltpu.make_async_remote_copy(
+                src_ref=mine if k == 0 else full(k), dst_ref=full(k), send_sem=sems.at[i], recv_sem=rsems.at[i],
+                device_id={"s": flip(me, to)}, device_id_type=pl.DeviceIdType.MESH,
+            )
+
+        self.direct = [copy(0, 0, first), copy(1, 0, second), copy(2, 0, 1)]
+        self.forward = [copy(3, first, second)]
+        self.core1 = [copy(4, first, 1), copy(5, second, 1)]
+        self.core2 = [copy(6, 6, 1)]
+
+
+def starts(cs):
+    for c in cs:
+        c().start()
+
+
+def begin(gathers):
+    for g in gathers:
+        starts(g.direct)
+
+
+def onward(gathers):
+    for g in gathers:
+        for c in g.direct[:2]:
+            c().wait_recv()
+        starts(g.forward)
+        starts(g.core1)
+
+
+def across(gathers):
+    for g in gathers:
+        g.forward[0]().wait_recv()
+        starts(g.core2)
+
+
+def here(gathers):
+    for g in gathers:
+        for c in g.direct[2:] + g.core1 + g.core2:
+            c().wait_recv()
+
+
+def sent(gathers):
+    for g in gathers:
+        for c in g.direct + g.forward + g.core1 + g.core2:
+            c().wait_send()
+
+
+def greet(me, others):
+    barrier = pltpu.get_barrier_semaphore()
+    for to in others:
+        pl.semaphore_signal(barrier, inc=1, device_id=to, device_id_type=pl.DeviceIdType.MESH)
+    pl.semaphore_wait(barrier, len(others))
+
+
+ORDER = ((4, 2), (2, 4))
+
+
 def forward_kernel(
-    x_ref, dy_ref, wg_hbm, wu_hbm, wd_hbm, at_ref, dyt_ref, g_ref, u_ref, hid_ref, wd_full, a_all, wg, wu, sems, rsems, own_sems
+    x_ref, dy_ref, wg_hbm, wu_hbm, wd_hbm, at_ref, dyt_ref, g_ref, u_ref, hid_ref, wd_full, wd_next, a_all, wg, wu, sems, rsems, own_sems
 ):
     me = lax.axis_index("s")
     j, t = pl.program_id(0), pl.program_id(1)
 
-    def copies(c, m):
-        first, second = ((4, 2), (2, 4))[m]
-
-        def part(ref, k, whole):
-            if c is None:
-                return ref.at[pl.ds(0 if whole else pl.multiple_of(flip(me, k) * 320, 64), 320), pl.ds(512 * m, 512)]
-            return ref.at[pl.ds(0 if whole else pl.multiple_of(flip(me, k) * 128, 128), 128), pl.ds(pl.multiple_of(c * FB, FB), FB)]
-
-        full = wd_full if c is None else (wg, wu)[m]
-        mine = wd_hbm.at[0] if c is None else (wg_hbm, wu_hbm)[m].at[0]
-        n = NJ if c is None else c
-
-        def copy(i, k, to):
-            src = part(mine, 0, True) if k == 0 else part(full, k, False)
-            return lambda: pltpu.make_async_remote_copy(
-                src_ref=src, dst_ref=part(full, k, False), send_sem=sems.at[n, m, i], recv_sem=rsems.at[n, m, i],
-                device_id={"s": flip(me, to)}, device_id_type=pl.DeviceIdType.MESH,
-            )
-
-        direct = [copy(0, 0, first), copy(1, 0, second), copy(2, 0, 1)]
-        forward = [copy(3, first, second)]
-        core = [copy(4, first, 1), copy(5, second, 1)], [copy(6, 6, 1)]
-        return direct, forward, core
-
-    def each(c, do):
-        for m in range(2):
-            do(*copies(c, m))
-
-    def starts(cs):
-        for x in cs:
-            x().start()
-
-    def begin(c):
-        each(c, lambda direct, forward, core: starts(direct))
-
-    def onward(c):
-        def do(direct, forward, core):
-            for x in direct[:2]:
-                x().wait_recv()
-            starts(forward)
-            starts(core[0])
-
-        each(c, do)
-
-    def across(c):
-        def do(direct, forward, core):
-            forward[0]().wait_recv()
-            starts(core[1])
-
-        each(c, do)
-
-    def here(c):
-        def do(direct, forward, core):
-            for x in direct[2:] + core[0] + core[1]:
-                x().wait_recv()
-
-        each(c, do)
-
-    def sent(c):
-        def do(direct, forward, core):
-            for x in direct + forward + core[0] + core[1]:
-                x().wait_send()
-
-        each(c, do)
-
-    def own():
-        rows = pl.ds(pl.multiple_of(me * 128, 128), 128)
-        down_rows = pl.ds(pl.multiple_of(me * 320, 64), 320)
-        return [
-            lambda: pltpu.make_async_copy(wg_hbm.at[0], wg.at[rows], own_sems.at[0]),
-            lambda: pltpu.make_async_copy(wu_hbm.at[0], wu.at[rows], own_sems.at[1]),
-            lambda: pltpu.make_async_copy(wd_hbm.at[0], wd_full.at[down_rows], own_sems.at[2]),
-        ]
+    def chunk(c):
+        cols = pl.ds(pl.multiple_of(c * FB, FB), FB)
+        out = []
+        for m in range(4):
+            if m < 2:
+                mine = (wg_hbm, wu_hbm)[m].at[0, :, cols]
+                full = lambda k, m=m: block((wg, wu)[m], pl.multiple_of(flip(me, k) * 128, 128), 128, cols)
+            else:
+                half = pl.ds(512 * (m - 2), 512)
+                mine = wd_hbm.at[0, pl.ds(pl.multiple_of(c * 64, 64), 64), half]
+                full = lambda k, half=half: block(wd_full, pl.multiple_of(flip(me, k) * 320 + c * 64, 64), 64, half)
+            out.append(Gather(me, mine, full, ORDER[m % 2], sems.at[c, m], rsems.at[c, m]))
+        return out
+
+    following = []
+    for m in range(2):
+        half = pl.ds(512 * m, 512)
+        full = lambda k, half=half: block(wd_next, pl.multiple_of(flip(me, k) * 320, 64), 320, half)
+        following.append(Gather(me, wd_hbm.at[1, :, half], full, ORDER[m], sems.at[NJ, m], rsems.at[NJ, m]))
+
+    rows = pl.ds(pl.multiple_of(me * 128, 128), 128)
+    down_rows = pl.ds(pl.multiple_of(me * 320, 64), 320)
+    own = [
+        lambda: pltpu.make_async_copy(wg_hbm.at[0], wg.at[rows], own_sems.at[0]),
+        lambda: pltpu.make_async_copy(wu_hbm.at[0], wu.at[rows], own_sems.at[1]),
+        lambda: pltpu.make_async_copy(wd_hbm.at[0], wd_full.at[down_rows], own_sems.at[2]),
+        lambda: pltpu.make_async_copy(wd_hbm.at[1], wd_next.at[down_rows], own_sems.at[3]),
+    ]
 
     @pl.when((j == 0) & (t == 0))
     def _():
-        barrier = pltpu.get_barrier_semaphore()
-        for k in (1, 2, 4):
-            pl.semaphore_signal(barrier, inc=1, device_id={"s": flip(me, k)}, device_id_type=pl.DeviceIdType.MESH)
-        pl.semaphore_wait(barrier, 3)
-        begin(0)
-        starts(own())
+        greet(me, [{"s": flip(me, k)} for k in (1, 2, 4)])
+        begin(chunk(0))
+        starts(own)
 
     @pl.when(j == 0)
     def _():
@@ -141,32 +159,32 @@
 
     @pl.when(((j == 0) & (t == 2)) | ((j > 0) & (j < NJ) & (t == 0)))
     def _():
-        onward(j)
+        onward(chunk(j))
 
         @pl.when(j < NJ - 1)
         def _():
-            begin(j + 1)
+            begin(chunk(j + 1))
 
         @pl.when(j == NJ - 1)
         def _():
-            begin(None)
+            begin(following)
 
     @pl.when(((j == 0) & (t == LAST)) | ((j > 0) & (j < NJ) & (t == 2)))
     def _():
-        across(j)
+        across(chunk(j))
 
     @pl.when((j < NJ) & (t == LAST))
     def _():
-        here(j)
+        here(chunk(j))
 
     @pl.when((j == 0) & (t == LAST))
     def _():
-        for x in own():
-            x().wait()
+        for c in own:
+            c().wait()
 
     @pl.when((j == NJ) & (t == 1))
     def _():
-        onward(None)
+        onward(following)
 
     @pl.when(j > 0)
     def _():
@@ -180,10 +198,10 @@
 
     @pl.when((j == NJ) & (t == LAST))
     def _():
-        across(None)
-        here(None)
-        sent(None)
-        lax.fori_loop(0, NJ, lambda c, _: (sent(c), 0)[1], 0)
+        across(following)
+        here(following)
+        sent(following)
+        lax.fori_loop(0, NJ, lambda c, _: (sent(chunk(c)), 0)[1], 0)
 
 
 def forward(x, dy, wg, wu, wd):
@@ -191,24 +209,54 @@
     cols = pl.BlockSpec((D, TT), lambda j, t: (0, jnp.where(j == 0, t, LAST)))
     tile = pl.BlockSpec((TT, FB), lambda j, t: (jnp.where(j == 0, 0, t), jnp.maximum(j - 1, 0)))
     anywhere = pl.BlockSpec(memory_space=pl.ANY)
-    sems = pltpu.SemaphoreType.DMA((NJ + 1, 2, 7))
+    sems = pltpu.SemaphoreType.DMA((NJ + 1, 4, 7))
     return pl.pallas_call(
         forward_kernel,
         cost_estimate=pl.CostEstimate(flops=4 * T * D * FF, bytes_accessed=10 * T * FF, transcendentals=0),
         compiler_params=pltpu.CompilerParams(vmem_limit_bytes=VMEM_LIMIT, collective_id=3, has_side_effects=True),
         name="forward", grid=(NJ + 1, T // TT),
-        in_specs=[rows, rows] + [anywhere] * 3, out_specs=[cols, cols, tile, tile, tile, anywhere],
+        in_specs=[rows, rows] + [anywhere] * 3, out_specs=[cols, cols, tile, tile, tile, anywhere, anywhere],
         out_shape=[
             jax.ShapeDtypeStruct((D, T), BF), jax.ShapeDtypeStruct((D, T), BF), jax.ShapeDtypeStruct((T, FF), F32),
             jax.ShapeDtypeStruct((T, FF), F32), jax.ShapeDtypeStruct((T, FF), BF), jax.ShapeDtypeStruct((FF, D), BF),
+            jax.ShapeDtypeStruct((FF, D), BF),
         ],
         scratch_shapes=[
-            pltpu.VMEM((T, D), BF), pltpu.VMEM((D, FF), BF), pltpu.VMEM((D, FF), BF), sems, sems, pltpu.SemaphoreType.DMA((3,)),
+            pltpu.VMEM((T, D), BF), pltpu.VMEM((D, FF), BF), pltpu.VMEM((D, FF), BF), sems, sems, pltpu.SemaphoreType.DMA((4,)),
         ],
     )(x, dy, wg, wu, wd)
 
 
-def down_kernel(hid_ref, x_ref, wd_ref, h_ref, a_ref, at_ref):
+def down_kernel(hid_ref, x_ref, wd_ref, wg_hbm, wu_hbm, h_ref, a_ref, at_ref, wg_next, wu_next, sems, rsems, own_sems):
+    me, t = lax.axis_index("s"), pl.program_id(0)
+    halves = []
+    for i in range(2):
+        cols = pl.ds(1280 * i, 1280)
+        halves.append([])
+        for m in range(2):
+            full = lambda k, m=m, cols=cols: block((wg_next, wu_next)[m], pl.multiple_of(flip(me, k) * 128, 128), 128, cols)
+            halves[i].append(Gather(me, (wg_hbm, wu_hbm)[m].at[1, :, cols], full, ORDER[m], sems.at[i, m], rsems.at[i, m]))
+    rows = pl.ds(pl.multiple_of(me * 128, 128), 128)
+    own = [
+        lambda: pltpu.make_async_copy(wg_hbm.at[1], wg_next.at[rows], own_sems.at[0]),
+        lambda: pltpu.make_async_copy(wu_hbm.at[1], wu_next.at[rows], own_sems.at[1]),
+    ]
+
+    @pl.when(t == 0)
+    def _():
+        greet(me, [{"s": flip(me, k)} for k in (1, 2, 4)])
+        begin(halves[0])
+        begin(halves[1])
+        starts(own)
+
+    @pl.when(t == 4)
+    def _():
+        onward(halves[0])
+
+    @pl.when(t == 7)
+    def _():
+        onward(halves[1])
+
     h = x_ref[...] + dot(hid_ref[...], wd_ref[...]).astype(BF)
     h_ref[...] = h
     wide = h.astype(F32)
@@ -216,15 +264,34 @@
     a_ref[...] = a
     at_ref[...] = a.T
 
-
-def down(hid, x, wd):
+    @pl.when(t == 7)
+    def _():
+        for g in halves:
+            across(g)
+        for g in halves:
+            here(g)
+            sent(g)
+        for c in own:
+            c().wait()
+
+
+def down(hid, x, wd, wg, wu):
     rows = pl.BlockSpec((512, D), lambda t: (t, 0))
-    return call(
-        down_kernel, 2 * T * D * FF, 2 * T * FF + 8 * T * D, name="down", grid=(T // 512,),
-        in_specs=[pl.BlockSpec((512, FF), lambda t: (t, 0)), rows, pl.BlockSpec((FF, D), lambda t: (0, 0))],
-        out_specs=[rows, rows, pl.BlockSpec((D, 512), lambda t: (0, t))],
-        out_shape=[jax.ShapeDtypeStruct((T, D), BF), jax.ShapeDtypeStruct((T, D), BF), jax.ShapeDtypeStruct((D, T), BF)],
-    )(hid, x, wd)
+    anywhere = pl.BlockSpec(memory_space=pl.ANY)
+    sems = pltpu.SemaphoreType.DMA((2, 2, 7))
+    return pl.pallas_call(
+        down_kernel,
+        cost_estimate=pl.CostEstimate(flops=2 * T * D * FF, bytes_accessed=2 * T * FF + 8 * T * D, transcendentals=0),
+        compiler_params=pltpu.CompilerParams(vmem_limit_bytes=VMEM_LIMIT, collective_id=4, has_side_effects=True),
+        name="down", grid=(T // 512,),
+        in_specs=[pl.BlockSpec((512, FF), lambda t: (t, 0)), rows, pl.BlockSpec((FF, D), lambda t: (0, 0)), anywhere, anywhere],
+        out_specs=[rows, rows, pl.BlockSpec((D, 512), lambda t: (0, t)), anywhere, anywhere],
+        out_shape=[
+            jax.ShapeDtypeStruct((T, D), BF), jax.ShapeDtypeStruct((T, D), BF), jax.ShapeDtypeStruct((D, T), BF),
+            jax.ShapeDtypeStruct((D, FF), BF), jax.ShapeDtypeStruct((D, FF), BF),
+        ],
+        scratch_shapes=[sems, sems, pltpu.SemaphoreType.DMA((2,))],
+    )(hid, x, wd, wg, wu)
 
 
 def cat(refs):
@@ -322,21 +389,34 @@
         dy_ref, at_ref, dyt_ref, wd_ref, out_ref, dg_ref, du_ref, hkeep, hsend, accg, accu, accd, down_ref, hsems, *comm = refs
     else:
         g_refs, u_refs, refs = refs[:4], refs[4:8], refs[8:]
-        dy_ref, at_ref, dyt_ref, wd_ref, hkeep, hsend, out_ref, accg, accu, accd, down_ref, hsems, *comm = refs
+        dy_ref, at_ref, dyt_ref, wd_ref, hkeep, hsend, done_ref, out_ref, sums_out, units_out, *refs = refs
+        accg, accu, accd, down_ref, hsems, squares, mine_ref, sums_ref, units_ref, tsems, trsems, *comm = refs
     keep, send1 = comm[:2]
     me, group = lax.axis_index("s"), lax.axis_index("r")
     j, t = pl.program_id(0), pl.program_id(1)
     last = pl.num_programs(1) - 1
     off = 0 if second else 1
-    s1, s2, s3, s4, final = exchange(me, 1 - group, *comm, out_ref)
+    s1, s2, s3, s4, last_stage = exchange(me, 1 - group, *comm, out_ref)
+
+    def square(v):
+        v = v.astype(F32)
+        squares[...] += jnp.sum((v * v).reshape(-1, 8, 512), axis=0)
+
+    def final(e, slot):
+        last_stage(e if second else e + NJ - 1, slot)
+        if not second:
+            square(out_ref[e + NJ - 1])
+
+    def copy_done():
+        return pltpu.make_async_copy(done_ref, out_ref.at[pl.ds(0, NJ - 1)], hsems.at[2])
+
 
     @pl.when((j == 0) & (t == 0))
     def _():
-        barrier = pltpu.get_barrier_semaphore()
-        for to in [{"s": flip(me, k)} for k in (1, 2, 4)] + [{"r": 1 - group}]:
-            pl.semaphore_signal(barrier, inc=1, device_id=to, device_id_type=pl.DeviceIdType.MESH)
-        pl.semaphore_wait(barrier, 4)
+        greet(me, [{"s": flip(me, k)} for k in ((1, 2, 4) if second else range(1, 8))] + [{"r": 1 - group}])
         if not second:
+            copy_done().start()
+            squares[...] = jnp.zeros_like(squares)
             hands = [pltpu.make_async_copy(hkeep, keep, hsems.at[0]), pltpu.make_async_copy(hsend, send1, hsems.at[1])]
             for h in hands:
                 h.start()
@@ -385,6 +465,13 @@
         def _():
             stage(slot)
 
+    if not second:
+        @pl.when((t == 1) & (j == 0))
+        def _():
+            copy_done().wait()
+            for i in range(NJ - 1):
+                square(out_ref[i])
+
     @pl.when((t == 1) & (e >= 1))
     def _():
         final(e - 1, lax.rem(e + 1, 2))
@@ -429,6 +516,31 @@
             for stage in (s2, s3, s4):
                 stage(NJ % 2)
             final(NJ, NJ % 2)
+            mine_ref[...] = sum(squares[:, 128 * i : 128 * (i + 1)] for i in range(4))
+            sums_ref[me] = mine_ref[...]
+            tails = [
+                pltpu.make_async_remote_copy(
+                    src_ref=mine_ref, dst_ref=sums_ref.at[me], send_sem=tsems.at[k], recv_sem=trsems.at[k],
+                    device_id={"s": flip(me, k)}, device_id_type=pl.DeviceIdType.MESH,
+                )
+                for k in range(1, 8)
+            ]
+            theirs = 3 - 3 * lax.rem(me, 2)
+            for layer in range(2):
+                for i in range(2):
+                    n = 8 + 2 * layer + i
+                    tails.append(
+                        pltpu.make_async_remote_copy(
+                            src_ref=out_ref.at[NJ * layer + theirs + i, pl.ds(256, 128)], dst_ref=units_ref.at[layer, i],
+                            send_sem=tsems.at[n], recv_sem=trsems.at[n], device_id={"s": flip(me, 1)}, device_id_type=pl.DeviceIdType.MESH,
+                        )
+                    )
+            for c in tails:
+                c.start()
+            for c in tails:
+                c.wait()
+            sums_out[...] = sums_ref[...]
+            units_out[...] = units_ref[...]
 
 
 def grads(gate_up_of, dy, at, dyt, wd, handed=None):
@@ -443,11 +555,12 @@
         g, u = gate_up_of
         gspec = [pl.BlockSpec((TT, 128), lambda j, t, c=c: (t, 5 * c + j)) for c in range(4)]
         ops, specs = [g] * 4 + [u] * 4, gspec * 2
-    chunks = NJ - 1 if second else NJ + 1
+    chunks = NJ - 1 if second else 2 * NJ
     ops += [dy, at, dyt, wd.reshape(4, NJ, 128, D)]
     specs += [rows, cols, cols, pl.BlockSpec((4, 1, 128, D), lambda j, t: (0, j, 0, 0))]
     outs = [jax.ShapeDtypeStruct((chunks, 384, 512), BF)]
     ospecs = [pl.BlockSpec((chunks, 384, 512), lambda j, t: (0, 0, 0))]
+    tail = []
     hand = [jax.ShapeDtypeStruct((2, 2, 384, 512), F32), jax.ShapeDtypeStruct((2, 2, 384, 512), BF)]
     anywhere = [pl.BlockSpec(memory_space=pl.ANY)] * 2
     if second:
@@ -455,14 +568,17 @@
         ospecs += [pl.BlockSpec((TT, FB), lambda j, t: (t, j))] * 2 + anywhere
     else:
         ops += handed
-        specs += anywhere
+        specs += anywhere + anywhere[:1]
+        outs += [jax.ShapeDtypeStruct((8, 8, 128), F32), jax.ShapeDtypeStruct((2, 2, 128, 512), BF)]
+        ospecs += [pl.BlockSpec((8, 8, 128), lambda j, t: (0, 0, 0)), pl.BlockSpec((2, 2, 128, 512), lambda j, t: (0, 0, 0, 0))]
+        tail = [pltpu.VMEM((8, 512), F32), pltpu.VMEM((8, 128), F32), pltpu.VMEM((8, 8, 128), F32), pltpu.VMEM((2, 2, 128, 512), BF), pltpu.SemaphoreType.DMA((12,)), pltpu.SemaphoreType.DMA((12,))]
     return pl.pallas_call(
         functools.partial(grads_kernel, second),
         cost_estimate=pl.CostEstimate(flops=(12 if second else 8) * T * D * FF, bytes_accessed=40 * T * D * NJ, transcendentals=0),
         compiler_params=pltpu.CompilerParams(vmem_limit_bytes=VMEM_LIMIT, collective_id=1 if second else 2, has_side_effects=True),
         name="grads_second" if second else "grads_first", grid=(NJ, T // TT),
         in_specs=specs, out_specs=ospecs, out_shape=outs,
-        scratch_shapes=[pltpu.VMEM((D, FB), F32)] * 3 + [pltpu.VMEM((FB, D), F32), pltpu.SemaphoreType.DMA((2,))] + comm_scratch(chunks),
+        scratch_shapes=[pltpu.VMEM((D, FB), F32)] * 3 + [pltpu.VMEM((FB, D), F32), pltpu.SemaphoreType.DMA((3,))] + tail + comm_scratch(chunks),
     )(*ops)
 
 
@@ -504,52 +620,61 @@
     )(*dgs, *dus, h, dy, wg, wu)
 
 
-def adamw(w, m, v, g):
-    m = 0.9 * m + 0.1 * g
-    v = 0.95 * v + 0.05 * g * g
-    step = m * lax.rsqrt(v + 1e-8) + 0.1 * w
-    return (w - 0.02 * step).astype(BF), m, v
+def update_kernel(g_ref, units_ref, sums_ref, *refs):
+    ins, outs = refs[:9], refs[9:]
+    layer, q = pl.program_id(0), pl.program_id(1)
+    core = lax.rem(lax.axis_index("s"), 2)
+    base = NJ * (1 - layer)
+    factor = jnp.minimum(1.0, 0.5 * lax.rsqrt(jnp.sum(sums_ref[...], keepdims=True)[0] * (1.0 / (3 * 2 * D * FF)) + 1e-30))
+
+    def wide(first):
+        parts = []
+        for b in range(4):
+            n = 4 * q + b
+            chip, c = lax.div(n, NJ), lax.rem(n, NJ)
+            parts.append(g_ref[base + c, first : first + 128, pl.ds(pl.multiple_of(chip * 128, 128), 128)])
+        return jnp.concatenate(parts, axis=1)
+
+    half = lax.div(q, 2)
+    own = g_ref[base + half + 2 * core, 256:384].astype(F32)
+    other = units_ref[1 - layer, jnp.minimum(half, 1)].astype(F32)
+    unit = jnp.where(lax.rem(q, 2) == 0, own, other)
+    grads = [wide(0).astype(F32), wide(128).astype(F32), jnp.concatenate([unit[:64], unit[64:]], axis=1)]
+    for i, g in enumerate(grads):
+        g = g * factor
+        w, m, v = (ins[3 * n + i][0].astype(F32) for n in range(3))
+        m = 0.9 * m + 0.1 * g
+        v = 0.95 * v + 0.05 * g * g
+        step = m * lax.rsqrt(v + 1e-8) + 0.1 * w
+        outs[i][0] = (w - 0.02 * step).astype(BF)
+        outs[3 + i][0] = m
+        outs[6 + i][0] = v
+
+
+def update(g, units, sums, arrays):
+    wide = pl.BlockSpec((1, 128, 512), lambda l, q: (l, 0, q))
+    tall = pl.BlockSpec((1, 64, D), lambda l, q: (l, q, 0))
+    specs = [wide, wide, tall] * 3
+    whole = [pl.BlockSpec(v.shape, lambda l, q, n=v.ndim: (0,) * n) for v in (g, units, sums)]
+    return pl.pallas_call(
+        update_kernel,
+        cost_estimate=pl.CostEstimate(flops=10 * 6 * D * FF // 8, bytes_accessed=20 * 6 * D * FF // 8, transcendentals=0),
+        compiler_params=pltpu.CompilerParams(vmem_limit_bytes=VMEM_LIMIT),
+        name="update", grid=(2, NJ), in_specs=whole + specs, out_specs=specs,
+        out_shape=[jax.ShapeDtypeStruct(v.shape, v.dtype) for v in arrays],
+    )(g, units, sums, *arrays)
 
 
 def solution(mesh):
-    size = mesh.shape["s"]
-
-    def swap(v, k):
-        return lax.ppermute(v, "s", [(i, i ^ k) for i in range(size)])
-
-    def gradients_of(parts):
-        whole = jnp.concatenate(parts, axis=0)
-        gate, up = (
-            whole[:, 128 * i : 128 * (i + 1)].reshape(NJ, 128, 4, 128).transpose(1, 2, 0, 3).reshape(128, FF) for i in range(2)
-        )
-        rows = jnp.concatenate([whole[:, 256:320], whole[:, 320:384]], axis=2)
-        core = lax.axis_index("s") % 2
-        mine = jnp.where(core == 0, rows[:3], rows[2:])
-        other = swap(jnp.where(core == 0, rows[3:], rows[:2]), 1)
-        units = jnp.stack([mine[0], other[0], mine[1], other[1], mine[2]])
-        return gate, up, units.reshape(320, D)
-
-    def fetched(weights, number):
-        return [lax.all_gather(w[number], "s", axis=0, tiled=True) for w in weights]
-
     def step(x, dy, *arrays):
-        weights, m, v = (arrays[i : i + 3] for i in (0, 3, 6))
-        x, dy = x[0], dy[0]
-        wg1, wu1, wd1 = fetched(weights, 1)
-        a0t, dyt, g0, u0, hid0, wd0 = forward(x, dy, *weights)
-        h1, a1, a1t = down(hid0, x, wd0)
+        weights, x, dy = arrays[:3], x[0], dy[0]
+        wg, wu, wd = weights
+        a0t, dyt, g0, u0, hid0, wd0, wd1 = forward(x, dy, *weights)
+        h1, a1, a1t, wg1, wu1 = down(hid0, x, wd0, wg, wu)
         done1, dg, du, *handed = grads((a1, wg1, wu1), dy, a1t, dyt, wd1)
         dh1, dh1t = dstate([dg], [du], h1, dy, wg1, wu1)
-        done0, = grads((g0, u0), dh1, a0t, dh1t, wd0, handed)
-        parts1, parts0 = [done1, done0[:1]], [done0[1:]]
-        both = [gradients_of(parts0), gradients_of(parts1)]
-        gs = [[both[l][i].astype(F32) for l in range(2)] for i in range(3)]
-        squares = lax.psum(sum(jnp.sum(g * g) for pair in gs for g in pair), "s")
-        factor = jnp.minimum(1.0, 0.5 * lax.rsqrt(squares / (3 * 2 * D * FF) + 1e-30))
-        new = [
-            adamw(w.astype(F32), mm, vv, jnp.stack(g) * factor) for w, mm, vv, g in zip(weights, m, v, gs, strict=True)
-        ]
-        return tuple(one[which] for which in range(3) for one in new)
+        done, sums, units = grads((g0, u0), dh1, a0t, dh1t, wd0, handed + [done1])
+        return tuple(update(done, units, sums, arrays))
 
     states, cut = P(("rep", "r", "s"), None, None), P(None, "s", None)
     return jax.shard_map(

time: 644 us -> 582 us (0.904)
  local copies, waits for them, and re-layouts: 57 us -> 0 us
  Pallas kernels: 531 us -> 581 us
  other arithmetic: 22.4 us -> 0 us
  between operations: 18.6 us -> 0.85 us
  blocking collectives: 13.3 us -> 0 us
    pallas_call x1 -> x2, Pallas kernels: 32.7 us -> 71.9 us  [the longest x1 52.7 us: down(): pl.pallas_call(down_kernel, cost_estimate=pl.CostEstimate(flops=2 * T * D...]
    unnamed x48 -> x0, local copies, waits for them, and re-layouts: 37.1 us -> none
    convert_element_type x3 -> x0, other arithmetic: 15.7 us -> none  [adamw(): return ((w - 0.02 * step).astype(BF), m, v)]
    psum x1 -> x0, blocking collectives: 13.3 us -> none  [step(): squares = lax.psum(sum((jnp.sum(g * g) for pair in gs for g in pair)), 's')]
    pallas_call x2, Pallas kernels: 318 us -> 328 us  [grads(): pl.pallas_call(functools.partial(grads_kernel, second), cost_estimate=pl....]
    convert_element_type x8 -> x0, local copies, waits for them, and re-layouts: 9.54 us -> none  [step(): gs = [[both[l][i].astype(F32) for l in range(2)] for i in range(3)]]
    slice x6 -> x0, local copies, waits for them, and re-layouts: 8.43 us -> none  [the longest x3 6.09 us: fetched(): return [lax.all_gather(w[number], 's', axis=0, tiled=True) for w in weights]]
  transfers between devices with their start and end apart: 5 -> 0, of which waited for: 0 -> 0; matrix products, arithmetic and copies ran while one was open for 5% -> 0% of each run, Pallas kernels for 24% -> 0%
where the time goes in v2:
time: 582 us
  Pallas kernels  581 us (100%)
    pallas_call x2, Pallas kernels, grads(): pl.pallas_call(functools.partial(grads_kernel, second), cost_estimate=pl....  328 us
    pallas_call x1, Pallas kernels, forward(): pl.pallas_call(forward_kernel, cost_estimate=pl.CostEstimate(flops=4 * T...  122 us
    pallas_call x1, Pallas kernels, dstate(): call(functools.partial(dstate_kernel, groups), 4 * T * D * FF, 4 * T * FF...  59.5 us
    pallas_call x1, Pallas kernels, down(): pl.pallas_call(down_kernel, cost_estimate=pl.CostEstimate(flops=2 * T * D...  52.7 us
    pallas_call x1, Pallas kernels, update(): pl.pallas_call(update_kernel, cost_estimate=pl.CostEstimate(flops=10 * 6...  19.2 us

profile of v2, /device:TPU:0, one launch (start us, length us, event | category | flops | bytes accessed | tf_op | source)
XLA Modules:
  0.0 581.7 jit_solution(17930708429180469059)
XLA Ops:
  0.6 121.6 %forward.1 = (bf16[1024,4096]{1,0:T(8,128)(2,1)}, bf16[1024,4096]{1,0:T(8,128)(2,1)}, f32[4096,2560]{1,0:T(8,128)}, f32[4096,2560]{1,0:T(8,128)}, bf16[4096,2560...) custom-call(bf16[4096,1024]{1,0:T(8,128)(2,1)} %bitcast.5, bf16[4096,1024]{1,0:T(8,128)(2,1)} %bitcast.7, ...), custom_call_target="tpu_custom_call" | custom-call | flops 42949672960 | bytes 104857600 | tf_op jit(solution)/shard_map/forward/pallas_call | solution.py:213
  122.2 52.7 %down.1 = (bf16[4096,1024]{1,0:T(8,128)(2,1)}, bf16[4096,1024]{1,0:T(8,128)(2,1)}, bf16[1024,4096]{1,0:T(8,128)(2,1)}, bf16[1024,2560]{1,0:T(8,128)(2,1)}, bf16[1024,2560]{1,0:T(8,128)(2,1)}) custom-call(bf16[4096,2560]{1,0:T(8,128)(2,1)} %get-tuple-element.33.hid_ref, bf16[4096,1024]{1,0:T(8,128)(2,1)} %bitcast.6, ...), custom_call_target="tpu_custom_call" | custom-call | flops 21474836480 | bytes 54525952 | tf_op jit(solution)/shard_map/down/pallas_call | solution.py:282
  174.9 169.5 %grads_second.1 = (bf16[4,384,512]{2,1,0:T(8,128)(2,1)}, bf16[4096,2560]{1,0:T(8,128)(2,1)}, bf16[4096,2560]{1,0:T(8,128)(2,1)}, f32[2,2,384,512]{3,2,1,0:T(8,128)}, bf16[2,2,384,512]{3,2,1,0:T(8,128)(2,1)}) custom-call(bf16[4096,1024]{1,0:T(8,128)(2,1)} %get-tuple-element.35.refs_0_, bf16[1024,2560]{1,0:T(8,128)(2,1)} %get-tuple-element.36.refs_1_.refs_2_.refs_3_.refs_4_, ...), custom_call_target="tpu_custom_call" | custom-call | flops 128849018880 | bytes 838860800 | tf_op jit(solution)/shard_map/grads_second/pallas_call | solution.py:575
  344.4 59.5 %dstate.1 = (bf16[4096,1024]{1,0:T(8,128)(2,1)}, bf16[1024,4096]{1,0:T(8,128)(2,1)}) custom-call(bf16[4096,2560]{1,0:T(8,128)(2,1)} %get-tuple-element.41.refs_0_, bf16[4096,2560]{1,0:T(8,128)(2,1)} %get-tuple-element.42.refs_1_, bf16[4096,1024]{1,0:T(8,128)(2,1)} %get-tuple-element.43.refs_2_, bf16[4096,1024]{1,0:T(8,128)(2,1)} %bitcast.9, ...), custom_call_target="tpu_custom_call" | custom-call | flops 42949672960 | bytes 75497472 | tf_op jit(solution)/shard_map/dstate/pallas_call | solution.py:615
  403.8 158.5 %grads_first.1 = (bf16[10,384,512]{2,1,0:T(8,128)(2,1)}, f32[8,8,128]{2,1,0:T(8,128)}, bf16[2,2,128,512]{3,2,1,0:T(8,128)(2,1)}) custom-call(f32[4096,2560]{1,0:T(8,128)} %get-tuple-element.31.refs_0_.refs_1_.refs_2_.refs_3_, f32[4096,2560]{1,0:T(8,128)} %get-tuple-element.31.refs_0_.refs_1_.refs_2_.refs_3_, ...), custom_call_target="tpu_custom_call" | custom-call | flops 85899345920 | bytes 838860800 | tf_op jit(solution)/shard_map/grads_first/pallas_call | solution.py:575
  562.3 19.2 %update.1 = (bf16[2,128,2560]{2,1,0:T(8,128)(2,1)}, bf16[2,128,2560]{2,1,0:T(8,128)(2,1)}, bf16[2,320,1024]{2,1,0:T(8,128)(2,1)}, f32[2,128,2560]{2,1,0:T(8,128)...) custom-call(bf16[10,384,512]{2,1,0:T(8,128)(2,1)} %get-tuple-element, ...), custom_call_target="tpu_custom_call" | custom-call | flops 19660800 | bytes 39321600 | tf_op jit(solution)/shard_map/update/pallas_call | solution.py:659
